TPU v7x, 32 devices: a whole 2x2x4 slice. The times are simulated.
32 devices in a mesh: band: 8 (over z, x), ga: 4 (over y, core).
Axes of the slice: x: 2, y: 2, z: 4, core: 2. Of those that a mesh axis runs over, the one named last changes fastest.
Arguments:
- elements: bfloat16 [2, 768, 2048], P(None, 'band', 'ga'), may hold values from -0.75 to 0.75
- screened: bfloat16 [2, 2, 2048, 2048], P(None, None, 'ga'), may hold values from -0.09375 to 0.09375
- energies: float32 [768], replicated, may hold values from -3 to 3
- freq_points: float32 [2], replicated, may hold values from -3 to 3
- freq_weights: float32 [2], replicated, may hold values from 0.5 to 2
- band_of_slot: int32 [768], replicated, may hold values from 0 to 767, each once
Outputs:
- sigma: float32 [2, 768, 768], P(None, 'band', 'ga')
Inputs may be any that keep to these rules, and one draw needn't show every extreme that they name: `band_of_slot`: each of 0 to 767 stands once.
All inputs are finite; a program needn't handle non-finite values.
Results may differ from a plain program's by a relative error of at most 0.0042.
Values may be sent and summed in bfloat16 or wider, within the bound.
No kernel may reach another device: no remote copies, remote signals or barrier semaphores. Data moves between devices by JAX's collectives and lax.ppermute only.
A program may use at most 128 MiB of HBM per device.

v0:
```python
import jax
import jax.numpy as jnp
from jax import lax
from jax.sharding import PartitionSpec as P


def make_left(block):
    flipped = jnp.stack([-block[1], block[0]])
    return jnp.stack([block, flipped])


def on_device(elements, screened, energies, freq_points, freq_weights, band_of_slot):
    bands = elements.shape[1]
    slot_energy = jnp.take(energies, band_of_slot)
    offset = slot_energy[None, :] - freq_points[:, None]
    screen = freq_weights[:, None] / (1.0 + 4.0 * offset * offset)
    own_start = lax.axis_index("band") * bands
    screen_own = lax.dynamic_slice_in_dim(screen, own_start, bands, 1)
    piece = lax.all_gather(elements, "ga", axis=2, tiled=True)
    real_side = jnp.stack([piece[0], -piece[1]])
    imag_side = jnp.stack([piece[1], piece[0]])
    sides = jnp.stack([real_side, imag_side])
    applied = jnp.einsum(
        "dcmk,wcgk->wdmg", sides, screened, preferred_element_type=jnp.float32
    ).astype(jnp.bfloat16)
    left_own = make_left(elements)
    pairs = jnp.einsum(
        "dcnk,wcmk->wdnm",
        left_own,
        lax.all_gather(applied, "band", axis=2, tiled=True),
        preferred_element_type=jnp.float32,
    )
    factor = 0.5 * (screen_own[:, :, None] + screen[:, None, :])
    partial_rows = jnp.sum(pairs * factor[:, None], axis=0)
    return lax.psum_scatter(partial_rows, "ga", scatter_dimension=2, tiled=True)


def solution(mesh):
    placed = (P(None, "band", "ga"), P(None, None, "ga", None), P(), P(), P(), P())
    return jax.shard_map(
        on_device, mesh=mesh, in_specs=placed, out_specs=P(None, "band", "ga"), check_vma=False
    )
```

profile of v0, /device:TPU:0, one launch (start us, length us, event | category | flops | bytes accessed | tf_op | source)
XLA Modules:
  0.0 121.1 jit_solution(2113868990376874802)
XLA Ops:
  6.5 0.0 copy-start
  6.5 0.0 all-gather.2.cloned.1.call-start
  6.5 10.4 %all_gather.6 = bf16[2,96,2048]{2,1,0:T(8,128)(2,1)S(1)} all-gather(bf16[2,96,512]{2,1,0:T(8,128)(2,1)} %param.6), channel_id=1, replica_groups=mesh['band'=8,'ga'=4] {'ga'}, dimensions={2}, use_global_device_ids=true | all-gather | bytes 983040 | tf_op jit(solution)/shard_map/all_gather | solution.py:19
  17.0 0.1 slice_negate_fusion.1
  17.1 0.1 maximum_bitcast_fusion.8
  17.2 0.0 copy-start.2
  17.2 7.0 %fusion.21 = bf16[2,2,96,512]{3,2,1,0:T(8,128)(2,1)} fusion(bf16[2,2,512,2048]{3,2,1,0:T(8,128)(2,1)} %param.7, bf16[1,2,96,2048]{3,2,1,0:T(8,128)(2,1)S(1)} %get-tuple-element.9, bf16[1,2,96,2048]{3,2,1,0:T(8,128)(2,1)S(1)} %get-tuple-element.8), kind=kOutput, calls=%fused_computation.13 | convolution fusion | flops 1613955072 | bytes 10354688 | tf_op jit(solution)/shard_map/dcmk,wcgk->wdmg/dot_general | solution.py:23
  24.2 0.0 copy-start.3
  24.2 0.0 copy-start.4
  24.2 0.0 copy-start.1
  24.2 0.0 all-gather.2.cloned.1.call-update
  24.3 0.0 reduce-scatter.4.cloned.1.call-start
  24.3 0.0 copy-done.2
  24.4 0.0 copy-done
  24.4 3.2 %gather_fusion = f32[768]{0:T(1024)S(1)} fusion(f32[768]{0:T(1024)S(1)} %copy-done, s32[1024]{0:T(1024)S(1)} %pad_clamp_fusion), kind=kCustom, calls=%fused_computation | custom fusion | bytes 9216 | tf_op jit(solution)/shard_map/jit(_take)/gather | solution.py:14
  27.6 0.0 copy-done.3
  27.6 0.0 copy-done.4
  27.6 0.1 fusion.27
  27.7 0.1 constant_dynamic-slice_fusion
  27.8 0.0 copy-done.1
  27.8 0.1 add_multiply_fusion
  27.9 57.3 %all-gather.2.cloned.1.call-done = bf16[2,2,768,512]{3,2,1,0:T(8,128)(2,1)} async-done(((bf16[2,2,96,512]{3,2,1,0:T(8,128)(2,1)}), bf16[2,2,768,512]{3,2,1,0:T(8,128)(2,1)}) %all-gather.2.cloned.1.call-update) | async-done | bytes 3145744 | tf_op jit(solution)/shard_map/all_gather | solution.py:30
  85.3 3.1 %fusion.12 = f32[2,96,768]{2,1,0:T(8,128)S(1)} fusion(bf16[2,2,768,512]{3,2,1,0:T(8,128)(2,1)} %all-gather.2.cloned.1.call-done, f32[2,96,768]{2,1,0:T(8,128)S(1)} %add_multiply_fusion, bf16[1,2,96,512]{3,2,1,0:T(8,128)(2,1)S(1)} %maximum_bitcast_fusion.12, bf16[1,2,96,512]{3,2,1,0:T(8,128)(2,1)S(1)} %bitcast.63), kind=kOutput, calls=%fused_computation.10 | convolution fusion | flops 605208576 | bytes 4718592 | tf_op jit(solution)/shard_map/dcnk,wcmk->wdnm/dot_general | solution.py:27
  88.4 0.5 copy.11
  88.9 1.4 %reshape.63 = f32[768,192]{1,0:T(8,128)} reshape(f32[768,2,96]{2,1,0:T(2,128)S(1)} %bitcast.61) | data formatting | bytes 1179648
  90.2 0.0 reduce-scatter.4.cloned.1.call-update
  90.3 22.0 %reduce-scatter.4.cloned.1.call-done = f32[192,192]{1,0:T(8,128)} async-done(((f32[768,192]{1,0:T(8,128)}), f32[192,192]{1,0:T(8,128)}) %reduce-scatter.4.cloned.1.call-update) | async-done | bytes 147472
  112.3 1.1 reshape.64
  113.4 0.8 copy.12
  (5 shorter events, 0.1 us)
Async XLA Ops:
  6.5 17.8 %copy-start = (f32[768]{0:T(1024)S(1)}, f32[768]{0:T(1024)}, u32[]{:S(2)}) copy-start(f32[768]{0:T(1024)} %param.8) | copy-start | bytes 9220
  6.5 78.7 %all-gather.2.cloned.1.call-start = ((), (), s32[]{:S(2)}) async-start(), calls=%async_computation.1 | async-start | bytes 3538944 | tf_op jit(solution)/shard_map/all_gather | solution.py:30
  17.2 7.1 %copy-start.2 = (s32[768]{0:T(1024)S(1)}, s32[768]{0:T(1024)}, u32[]{:S(2)}) copy-start(s32[768]{0:T(1024)} %param.11) | copy-start | bytes 9220
  24.2 3.3 %copy-start.3 = (f32[2]{0:T(128)S(1)}, f32[2]{0:T(128)}, u32[]{:S(2)}) copy-start(f32[2]{0:T(128)} %param.10) | copy-start | bytes 28
  24.2 3.4 %copy-start.4 = (f32[2]{0:T(128)S(1)}, f32[2]{0:T(128)}, u32[]{:S(2)}) copy-start(f32[2]{0:T(128)} %param.9) | copy-start | bytes 28
  24.2 3.5 %copy-start.1 = (bf16[2,96,512]{2,1,0:T(8,128)(2,1)S(1)}, bf16[2,96,512]{2,1,0:T(8,128)(2,1)}, u32[]{:S(2)}) copy-start(bf16[2,96,512]{2,1,0:T(8,128)(2,1)} %param.6) | copy-start | bytes 589828
  24.3 88.0 %reduce-scatter.4.cloned.1.call-start = ((), (), s32[]{:S(2)}) async-start(), calls=%async_computation.2 | async-start | bytes 983040
Sparse Core Ops, SparseCore 0:
  24.4 60.8 all-gather.1
  90.4 21.8 reduce-scatter.3
where the time goes:
time: 121 us
  waiting for transfers between devices  79.4 us (66%)
  between operations  13.5 us (11%)
  blocking collectives  10.4 us (9%)
  matrix products  10.2 us (8%)
  local copies, waits for them, and re-layouts  7.04 us (6%)
    all_gather x1, waiting for transfers between devices, on_device(): lax.all_gather(applied, 'band', axis=2, tiled=True)  57.3 us
    unnamed x3, waiting for transfers between devices  22.1 us
    all_gather x1, blocking collectives, on_device(): piece = lax.all_gather(elements, 'ga', axis=2, tiled=True)  10.4 us
    dot_general x1, matrix products, on_device(): jnp.einsum('dcmk,wcgk->wdmg', sides, screened, preferred_element_type=jnp...  7.03 us
    unnamed x14, local copies, waits for them, and re-layouts  3.77 us
    gather x1, local copies, waits for them, and re-layouts, on_device(): slot_energy = jnp.take(energies, band_of_slot)  3.19 us
    dot_general x1, matrix products, on_device(): jnp.einsum('dcnk,wcmk->wdnm', left_own, lax.all_gather(applied, 'band', a...  3.12 us
  transfers between devices with their start and end apart: 2, of which 2 were waited for; matrix products, arithmetic and copies ran while one was open for 3% of the time, Pallas kernels for 0%

commit v1 on v0

--- a/solution.py
+++ b/solution.py
@@ -2,6 +2,21 @@
 import jax.numpy as jnp
 from jax import lax
 from jax.sharding import PartitionSpec as P
+
+
+def on_each_block(array, axis, dim, make, out_dim):
+    ways, here, step = (lax.axis_size(axis), lax.axis_index(axis), array.shape[dim])
+    results = []
+    for far in range(ways):
+        arriving = (
+            lax.ppermute(array, axis, [(d, (d + 1) % ways) for d in range(ways)])
+            if far + 1 < ways
+            else array
+        )
+        results.append(make(array, (here - far) % ways * step))
+        array = arriving
+    line = jnp.concatenate(results[::-1], axis=out_dim)
+    return jnp.roll(line, (here + 1) * results[0].shape[out_dim], axis=out_dim)
 
 
 def make_left(block):
@@ -24,11 +39,14 @@
         "dcmk,wcgk->wdmg", sides, screened, preferred_element_type=jnp.float32
     ).astype(jnp.bfloat16)
     left_own = make_left(elements)
-    pairs = jnp.einsum(
-        "dcnk,wcmk->wdnm",
-        left_own,
-        lax.all_gather(applied, "band", axis=2, tiled=True),
-        preferred_element_type=jnp.float32,
+    pairs = on_each_block(
+        applied,
+        "band",
+        2,
+        lambda own_block, offset_2: jnp.einsum(
+            "dcnk,wcmk->wdnm", left_own, own_block, preferred_element_type=jnp.float32
+        ),
+        3,
     )
     factor = 0.5 * (screen_own[:, :, None] + screen[:, None, :])
     partial_rows = jnp.sum(pairs * factor[:, None], axis=0)

time: 121 us -> 143 us (1.18)
  waiting for transfers between devices: 79.4 us -> 93.4 us
  local copies, waits for them, and re-layouts: 7.04 us -> 10.2 us
  matrix products: 10.2 us -> 12.1 us
  starting transfers between devices: 0.04 us -> 1.57 us
    ppermute x0 -> x7, waiting for transfers between devices: none -> 73.2 us  [on_each_block(): lax.ppermute(array, axis, [(d, (d + 1) % ways) for d in range(ways)])]
    all_gather x1 -> x0, waiting for transfers between devices: 57.3 us -> none  [on_device(): lax.all_gather(applied, 'band', axis=2, tiled=True)]
    concatenate x0 -> x1, local copies, waits for them, and re-layouts: none -> 3.15 us  [on_each_block(): return jnp.roll(line, (here + 1) * results[0].shape[out_dim], axis=out_dim)]
    dot_general x1 -> x8, matrix products: 3.12 us -> 5.87 us  [on_device(): jnp.einsum('dcnk,wcmk->wdnm', left_own, own_block, preferred_element_type...]
    unnamed x3 -> x2, waiting for transfers between devices: 22.1 us -> 20.3 us
    ppermute x0 -> x7, starting transfers between devices: none -> 1.57 us  [on_each_block(): lax.ppermute(array, axis, [(d, (d + 1) % ways) for d in range(ways)])]
    unnamed x14 -> x18, local copies, waits for them, and re-layouts: 3.77 us -> 3.81 us
  transfers between devices with their start and end apart: 2 -> 8, of which waited for: 2 -> 8; matrix products, arithmetic and copies ran while one was open for 3% -> 6% of each run, Pallas kernels for 0% -> 0%
where the time goes in v1:
time: 143 us; the launch traced here: 142 us
  waiting for transfers between devices  93.4 us (65%)
  between operations  13.6 us (10%)
  matrix products  12.1 us (8%)
  blocking collectives  10.4 us (7%)
  local copies, waits for them, and re-layouts  10.2 us (7%)
  starting transfers between devices  1.57 us (1%)
    ppermute x7, waiting for transfers between devices, on_each_block(): lax.ppermute(array, axis, [(d, (d + 1) % ways) for d in range(ways)])  73.2 us
    unnamed x2, waiting for transfers between devices  20.3 us
    all_gather x1, blocking collectives, on_device(): piece = lax.all_gather(elements, 'ga', axis=2, tiled=True)  10.4 us
    dot_general x1, matrix products, on_device(): jnp.einsum('dcmk,wcgk->wdmg', sides, screened, preferred_element_type=jnp...  6.28 us
    dot_general x8, matrix products, on_device(): jnp.einsum('dcnk,wcmk->wdnm', left_own, own_block, preferred_element_type...  5.87 us
    unnamed x18, local copies, waits for them, and re-layouts  3.81 us
    gather x1, local copies, waits for them, and re-layouts, on_device(): slot_energy = jnp.take(energies, band_of_slot)  3.19 us
    concatenate x1, local copies, waits for them, and re-layouts, on_each_block(): return jnp.roll(line, (here + 1) * results[0].shape[out_dim], axis=out_dim)  3.15 us
  transfers between devices with their start and end apart: 8, of which 8 were waited for; matrix products, arithmetic and copies ran while one was open for 6% of the time, Pallas kernels for 0%

profile of v1, /device:TPU:0, one launch (start us, length us, event | category | flops | bytes accessed | tf_op | source)
XLA Modules:
  0.0 142.2 jit_solution(1200504000061221668)
XLA Ops:
  6.5 0.0 copy-start
  6.5 0.0 reduce-scatter.4.cloned.1.call-start
  6.5 10.4 %all_gather.3 = bf16[2,96,2048]{2,1,0:T(8,128)(2,1)S(1)} all-gather(bf16[2,96,512]{2,1,0:T(8,128)(2,1)} %param.6), channel_id=1, replica_groups=mesh['band'=8,'ga'=4] {'ga'}, dimensions={2}, use_global_device_ids=true | all-gather | bytes 983040 | tf_op jit(solution)/shard_map/all_gather | solution.py:34
  17.0 0.1 slice_negate_fusion.1
  17.1 0.1 maximum_bitcast_fusion.6
  17.2 0.0 copy-start.2
  17.2 6.3 %fusion.7 = bf16[2,96,2,512]{3,1,2,0:T(8,128)(2,1)S(1)} fusion(bf16[2,2,512,2048]{3,2,1,0:T(8,128)(2,1)} %param.7, bf16[1,2,96,2048]{3,2,1,0:T(8,128)(2,1)S(1)} %get-tuple-element.9, bf16[1,2,96,2048]{3,2,1,0:T(8,128)(2,1)S(1)} %get-tuple-element.8), kind=kOutput, calls=%fused_computation.7 | convolution fusion | flops 1613955072 | bytes 10354688 | tf_op jit(solution)/shard_map/dcmk,wcgk->wdmg/dot_general | solution.py:38
  23.5 0.0 copy-start.3
  23.5 0.0 copy-start.4
  23.5 0.0 copy-start.1
  23.5 1.6 %collective-permute-start = (bf16[2,2,96,512]{3,2,0,1:T(8,128)(2,1)S(1)}, bf16[2,2,96,512]{3,2,0,1:T(8,128)(2,1)S(1)}, u32[]{:S(2)}, u32[]{:S(2)}) collective-permute-start(bf16[2,2,96,512]{3,2,0,1:T(8,128)(2,1)S(1)} %bitcast.124), channel_id=1, source_target_pairs={{0,4},{4,8},{8,12},{12,16},{16,20},{20,24},{24,28},{28,0},{1,5},{5... | collective-permute-start | bytes 1179656 | tf_op jit(solution)/shard_map/ppermute | solution.py:12
  25.1 12.7 %collective-permute-done = bf16[2,2,96,512]{3,2,0,1:T(8,128)(2,1)S(1)} collective-permute-done((bf16[2,2,96,512]{3,2,0,1:T(8,128)(2,1)S(1)}, bf16[2,2,96,512]{3,2,0,1:T(8,128)(2,1)S(1)}, u32[]{:S(2)}, u32[]{:S(2)}) %collective-permute-start) | collective-permute-done | bytes 393248 | tf_op jit(solution)/shard_map/ppermute | solution.py:12
  37.7 0.0 collective-permute-start.1
  37.7 0.0 copy-done.2
  37.8 0.0 copy-done
  37.8 3.2 %gather_fusion = f32[768]{0:T(1024)S(1)} fusion(f32[768]{0:T(1024)S(1)} %copy-done, s32[1024]{0:T(1024)S(1)} %pad_clamp_fusion), kind=kCustom, calls=%fused_computation | custom fusion | bytes 9216 | tf_op jit(solution)/shard_map/jit(_take)/gather | solution.py:29
  41.0 10.1 %collective-permute-done.1 = bf16[2,2,96,512]{3,2,0,1:T(8,128)(2,1)S(1)} collective-permute-done((bf16[2,2,96,512]{3,2,0,1:T(8,128)(2,1)S(1)}, bf16[2,2,96,512]{3,2,0,1:T(8,128)(2,1)S(1)}, u32[]{:S(2)}, u32[]{:S(2)}) %collective-permute-start.1) | collective-permute-done | bytes 393248 | tf_op jit(solution)/shard_map/ppermute | solution.py:12
  51.0 0.0 collective-permute-start.2
  51.1 0.0 copy-done.3
  51.1 0.0 copy-done.4
  51.1 0.1 fusion.19
  51.2 12.3 %collective-permute-done.2 = bf16[2,2,96,512]{3,2,0,1:T(8,128)(2,1)S(1)} collective-permute-done((bf16[2,2,96,512]{3,2,0,1:T(8,128)(2,1)S(1)}, bf16[2,2,96,512]{3,2,0,1:T(8,128)(2,1)S(1)}, u32[]{:S(2)}, u32[]{:S(2)}) %collective-permute-start.2) | collective-permute-done | bytes 393248 | tf_op jit(solution)/shard_map/ppermute | solution.py:12
  63.5 0.0 collective-permute-start.3
  63.5 0.1 constant_dynamic-slice_fusion
  63.6 0.0 copy-done.1
  63.6 11.5 %collective-permute-done.3 = bf16[2,2,96,512]{3,2,0,1:T(8,128)(2,1)S(1)} collective-permute-done((bf16[2,2,96,512]{3,2,0,1:T(8,128)(2,1)S(1)}, bf16[2,2,96,512]{3,2,0,1:T(8,128)(2,1)S(1)}, u32[]{:S(2)}, u32[]{:S(2)}) %collective-permute-start.3) | collective-permute-done | bytes 393248 | tf_op jit(solution)/shard_map/ppermute | solution.py:12
  75.1 0.0 copy-start.5
  75.1 0.0 collective-permute-start.4
  75.1 0.3 convolution_bitcast_fusion
  75.4 0.1 add_multiply_fusion
  75.5 10.3 %collective-permute-done.4 = bf16[2,2,96,512]{3,2,0,1:T(8,128)(2,1)S(1)} collective-permute-done((bf16[2,2,96,512]{3,2,0,1:T(8,128)(2,1)S(1)}, bf16[2,2,96,512]{3,2,0,1:T(8,128)(2,1)S(1)}, u32[]{:S(2)}, u32[]{:S(2)}) %collective-permute-start.4) | collective-permute-done | bytes 393248 | tf_op jit(solution)/shard_map/ppermute | solution.py:12
  85.8 0.0 copy-done.5
  85.8 0.0 collective-permute-start.5
  85.8 0.0 copy-start.6
  85.8 0.3 convolution_bitcast_fusion.1
  86.1 0.3 convolution_bitcast_fusion.2
  86.5 1.0 convolution_bitcast_fusion.3
  87.4 8.9 %collective-permute-done.5 = bf16[2,2,96,512]{3,2,0,1:T(8,128)(2,1)S(1)} collective-permute-done((bf16[2,2,96,512]{3,2,0,1:T(8,128)(2,1)S(1)}, bf16[2,2,96,512]{3,2,0,1:T(8,128)(2,1)S(1)}, u32[]{:S(2)}, u32[]{:S(2)}) %collective-permute-start.5) | collective-permute-done | bytes 393248 | tf_op jit(solution)/shard_map/ppermute | solution.py:12
  96.3 0.0 collective-permute-start.6
  96.3 0.0 copy-done.6
  96.3 1.0 convolution_bitcast_fusion.4
  97.3 1.0 convolution_bitcast_fusion.5
  98.3 1.0 convolution_bitcast_fusion.6
  99.3 7.5 %collective-permute-done.6 = bf16[2,2,96,512]{3,2,0,1:T(8,128)(2,1)S(1)} collective-permute-done((bf16[2,2,96,512]{3,2,0,1:T(8,128)(2,1)S(1)}, bf16[2,2,96,512]{3,2,0,1:T(8,128)(2,1)S(1)}, u32[]{:S(2)}, u32[]{:S(2)}) %collective-permute-start.6) | collective-permute-done | bytes 393248 | tf_op jit(solution)/shard_map/ppermute | solution.py:12
  106.8 1.0 convolution_bitcast_fusion.7
  107.8 3.1 %concatenate.6 = f32[2,2,96,1536]{3,2,1,0:T(8,128)S(1)} concatenate(f32[2,2,96,96]{3,2,1,0:T(8,128)} %convolution_bitcast_fusion.7, f32[2,2,96,96]{3,2,1,0:T(8,128)} %convolution_bitcast_fusion.6, f32[2,2,96,96]{3,2,1,0:T(8,128)} %convolution_bitcast_fusion.5, f32[2,2,96,96]{3,2,1,0:T(8,128)} %convolution_bitcast_fusion.4, f32[2,2,96,96]{3,2,1,0:T(8,128)} %convolution_bitcast_fusion.3, ...), dimensions={3} | concatenate | bytes 4718592 | tf_op jit(solution)/shard_map/jit(_roll_dynamic)/concatenate | solution.py:19
  110.9 0.4 multiply_reduce_fusion
  111.3 0.5 copy.65
  111.8 1.4 reshape.77
  113.2 0.0 reduce-scatter.4.cloned.1.call-update
  113.2 20.3 %reduce-scatter.4.cloned.1.call-done = f32[192,192]{1,0:T(8,128)} async-done(((f32[768,192]{1,0:T(8,128)}), f32[192,192]{1,0:T(8,128)}) %reduce-scatter.4.cloned.1.call-update) | async-done | bytes 147472
  133.4 1.1 reshape.78
  134.5 0.8 copy.66
  (5 shorter events, 0.0 us)
Async XLA Ops:
  6.5 31.2 %copy-start = (f32[768]{0:T(1024)S(1)}, f32[768]{0:T(1024)}, u32[]{:S(2)}) copy-start(f32[768]{0:T(1024)} %param.8) | copy-start | bytes 9220
  6.5 126.9 %reduce-scatter.4.cloned.1.call-start = ((), (), s32[]{:S(2)}) async-start(), calls=%async_computation.1 | async-start | bytes 983040
  17.2 20.6 %copy-start.2 = (s32[768]{0:T(1024)S(1)}, s32[768]{0:T(1024)}, u32[]{:S(2)}) copy-start(s32[768]{0:T(1024)} %param.11) | copy-start | bytes 9220
  23.5 27.6 %copy-start.3 = (f32[2]{0:T(128)S(1)}, f32[2]{0:T(128)}, u32[]{:S(2)}) copy-start(f32[2]{0:T(128)} %param.10) | copy-start | bytes 28
  23.5 27.6 %copy-start.4 = (f32[2]{0:T(128)S(1)}, f32[2]{0:T(128)}, u32[]{:S(2)}) copy-start(f32[2]{0:T(128)} %param.9) | copy-start | bytes 28
  23.5 40.0 %copy-start.1 = (bf16[2,96,512]{2,1,0:T(8,128)(2,1)S(1)}, bf16[2,96,512]{2,1,0:T(8,128)(2,1)}, u32[]{:S(2)}) copy-start(bf16[2,96,512]{2,1,0:T(8,128)(2,1)} %param.6) | copy-start | bytes 589828
  23.5 14.2 %collective-permute-start = (bf16[2,2,96,512]{3,2,0,1:T(8,128)(2,1)S(1)}, bf16[2,2,96,512]{3,2,0,1:T(8,128)(2,1)S(1)}, u32[]{:S(2)}, u32[]{:S(2)}) collective-permute-start(bf16[2,2,96,512]{3,2,0,1:T(8,128)(2,1)S(1)} %bitcast.124), channel_id=1, source_target_pairs={{0,4},{4,8},{8,12},{12,16},{16,20},{20,24},{24,28},{28,0},{1,5},{5... | collective-permute-start | bytes 1179656 | tf_op jit(solution)/shard_map/ppermute | solution.py:12
  37.7 13.3 %collective-permute-start.1 = (bf16[2,2,96,512]{3,2,0,1:T(8,128)(2,1)S(1)}, bf16[2,2,96,512]{3,2,0,1:T(8,128)(2,1)S(1)}, u32[]{:S(2)}, u32[]{:S(2)}) collective-permute-start(bf16[2,2,96,512]{3,2,0,1:T(8,128)(2,1)S(1)} %collective-permute-done), channel_id=1, source_target_pairs={{0,4},{4,8},{8,12},{12,16},{16,20},{20,24},{24,28},{28,0},{1,5},{5... | collective-permute-start | bytes 1179656 | tf_op jit(solution)/shard_map/ppermute | solution.py:12
  51.0 12.4 %collective-permute-start.2 = (bf16[2,2,96,512]{3,2,0,1:T(8,128)(2,1)S(1)}, bf16[2,2,96,512]{3,2,0,1:T(8,128)(2,1)S(1)}, u32[]{:S(2)}, u32[]{:S(2)}) collective-permute-start(bf16[2,2,96,512]{3,2,0,1:T(8,128)(2,1)S(1)} %collective-permute-done.1), channel_id=1, source_target_pairs={{0,4},{4,8},{8,12},{12,16},{16,20},{20,24},{24,28},{28,0},{1,5},{5... | collective-permute-start | bytes 1179656 | tf_op jit(solution)/shard_map/ppermute | solution.py:12
  63.5 11.6 %collective-permute-start.3 = (bf16[2,2,96,512]{3,2,0,1:T(8,128)(2,1)S(1)}, bf16[2,2,96,512]{3,2,0,1:T(8,128)(2,1)S(1)}, u32[]{:S(2)}, u32[]{:S(2)}) collective-permute-start(bf16[2,2,96,512]{3,2,0,1:T(8,128)(2,1)S(1)} %collective-permute-done.2), channel_id=1, source_target_pairs={{0,4},{4,8},{8,12},{12,16},{16,20},{20,24},{24,28},{28,0},{1,5},{5... | collective-permute-start | bytes 1179656 | tf_op jit(solution)/shard_map/ppermute | solution.py:12
  75.1 10.7 %copy-start.5 = (bf16[2,2,96,512]{3,2,0,1:T(8,128)(2,1)}, bf16[2,2,96,512]{3,2,0,1:T(8,128)(2,1)S(1)}, u32[]{:S(2)}) copy-start(bf16[2,2,96,512]{3,2,0,1:T(8,128)(2,1)S(1)} %collective-permute-done.3) | copy-start | bytes 1179652
  75.1 10.7 %collective-permute-start.4 = (bf16[2,2,96,512]{3,2,0,1:T(8,128)(2,1)S(1)}, bf16[2,2,96,512]{3,2,0,1:T(8,128)(2,1)S(1)}, u32[]{:S(2)}, u32[]{:S(2)}) collective-permute-start(bf16[2,2,96,512]{3,2,0,1:T(8,128)(2,1)S(1)} %collective-permute-done.3), channel_id=1, source_target_pairs={{0,4},{4,8},{8,12},{12,16},{16,20},{20,24},{24,28},{28,0},{1,5},{5... | collective-permute-start | bytes 1179656 | tf_op jit(solution)/shard_map/ppermute | solution.py:12
  85.8 10.5 %collective-permute-start.5 = (bf16[2,2,96,512]{3,2,0,1:T(8,128)(2,1)S(1)}, bf16[2,2,96,512]{3,2,0,1:T(8,128)(2,1)S(1)}, u32[]{:S(2)}, u32[]{:S(2)}) collective-permute-start(bf16[2,2,96,512]{3,2,0,1:T(8,128)(2,1)S(1)} %collective-permute-done.4), channel_id=1, source_target_pairs={{0,4},{4,8},{8,12},{12,16},{16,20},{20,24},{24,28},{28,0},{1,5},{5... | collective-permute-start | bytes 1179656 | tf_op jit(solution)/shard_map/ppermute | solution.py:12
  85.8 10.5 %copy-start.6 = (bf16[2,2,96,512]{3,2,0,1:T(8,128)(2,1)S(1)}, bf16[2,2,96,512]{3,2,0,1:T(8,128)(2,1)}, u32[]{:S(2)}) copy-start(bf16[2,2,96,512]{3,2,0,1:T(8,128)(2,1)} %copy-done.5) | copy-start | bytes 1179652
  96.3 10.5 %collective-permute-start.6 = (bf16[2,2,96,512]{3,2,0,1:T(8,128)(2,1)S(1)}, bf16[2,2,96,512]{3,2,0,1:T(8,128)(2,1)S(1)}, u32[]{:S(2)}, u32[]{:S(2)}) collective-permute-start(bf16[2,2,96,512]{3,2,0,1:T(8,128)(2,1)S(1)} %collective-permute-done.5), channel_id=1, source_target_pairs={{0,4},{4,8},{8,12},{12,16},{16,20},{20,24},{24,28},{28,0},{1,5},{5... | collective-permute-start | bytes 1179656 | tf_op jit(solution)/shard_map/ppermute | solution.py:12
Sparse Core Ops, SparseCore 0:
  113.3 20.0 reduce-scatter.3
